TPU v7x, 32 devices: a whole 2x2x4 slice. The times are simulated.
32 devices in a mesh: cube: 2 (over y), gz: 8 (over z, x), gy: 2 (over core).
Axes of the slice: x: 2, y: 2, z: 4, core: 2. Of those that a mesh axis runs over, the one named last changes fastest.
Arguments:
- noisy_cube: float32 [64, 64, 256], P(('cube', 'gz'), 'gy'), parts along dimension 0, may hold values from -40 to 40
- thresholds: float32 [4], replicated, may hold values from 0.5 to 4
Outputs:
- denoised: float32 [64, 4, 64, 256], P(('cube', 'gz'), None, 'gy'), parts along dimension 0
- gcv_score: float32 [8], P('cube'), parts along dimension 0
There are 2 independent parts, one for each index of `cube`. A program takes and returns all parts, laid end to end along the dimension named above; an argument that names none is the same for every part. Nothing has to cross between parts.
All inputs are finite; a program needn't handle non-finite values.
Results may differ from a plain program's by a relative error of at most 0.0003.
Values sent between devices are 32-bit elements; how exact they have to be, the bound alone decides.
No kernel may reach another device: no remote copies, remote signals or barrier semaphores. Data moves between devices by JAX's collectives and lax.ppermute only.
A program may use at most 64 MiB of HBM per device.

v0:
```python
import jax
import jax.numpy as jnp
from jax import lax
from jax.sharding import PartitionSpec as P

LOWPASS = (
    0.2303778133088964,
    0.7148465705529155,
    0.6308807679298587,
    -0.0279837694168599,
    -0.1870348117190931,
    0.0308413818355607,
    0.0328830116668852,
    -0.010597401785069,
)
HIGHPASS = tuple(((-1) ** tap_index * LOWPASS[7 - tap_index] for tap_index in range(8)))
lead_taps = 6
trail_taps = 3


def passed_along(array, axis, by):
    devices = lax.axis_size(axis)
    return lax.ppermute(array, axis, [(i, (i + by) % devices) for i in range(devices)])


def analyse(extended, dimension_number, axis_length):
    lowband = 0.0
    highband = 0.0
    for tap_index in range(8):
        sliced = lax.slice_in_dim(
            extended, tap_index, tap_index + axis_length - 1, 2, dimension_number
        )
        lowband = lowband + LOWPASS[tap_index] * sliced
        highband = highband + HIGHPASS[tap_index] * sliced
    return (lowband, highband)


def synthesise(lowband, highband, dimension_number, axis_length):
    even_part = 0.0
    odd_part = 0.0
    for tap_index in range(4):
        low_slice = lax.slice_in_dim(
            lowband, 3 - tap_index, 3 - tap_index + axis_length, 1, dimension_number
        )
        high_slice = lax.slice_in_dim(
            highband, 3 - tap_index, 3 - tap_index + axis_length, 1, dimension_number
        )
        even_part = (
            even_part + LOWPASS[2 * tap_index] * low_slice + HIGHPASS[2 * tap_index] * high_slice
        )
        odd_part = (
            odd_part
            + LOWPASS[2 * tap_index + 1] * low_slice
            + HIGHPASS[2 * tap_index + 1] * high_slice
        )
    paired = jnp.stack([even_part, odd_part], dimension_number + 1)
    target = list(even_part.shape)
    target[dimension_number] = 2 * axis_length
    return paired.reshape(target)


def merge_bands(lowband, highband):
    stacked = jnp.stack([lowband, highband], 2)
    return stacked.reshape((lowband.shape[0], 2 * lowband.shape[1]) + lowband.shape[2:])


def split_bands(current):
    halves = current.reshape((current.shape[0], current.shape[1] // 2, 2) + current.shape[2:])
    return (halves[:, :, 0], halves[:, :, 1])


def wrap_ahead(input_tensor, dimension_number, border_extent):
    return jnp.concatenate(
        [input_tensor, lax.slice_in_dim(input_tensor, 0, border_extent, 1, dimension_number)],
        dimension_number,
    )


def wrap_behind(input_tensor, dimension_number, border_extent):
    axis_length = input_tensor.shape[dimension_number]
    return jnp.concatenate(
        [
            lax.slice_in_dim(
                input_tensor, axis_length - border_extent, axis_length, 1, dimension_number
            ),
            input_tensor,
        ],
        dimension_number,
    )


def z_shift(input_tensor, start_offset):
    return passed_along(input_tensor, "gz", start_offset)


def y_shift(input_tensor, start_offset):
    return passed_along(input_tensor, "gy", start_offset)


def following_panel(input_tensor, dimension_number, border_extent, holding_tensor):
    axis_length = input_tensor.shape[dimension_number]
    split_pieces = [input_tensor]
    covered = 0
    start_offset = 1
    while covered < border_extent:
        shift_amount = min(axis_length, border_extent - covered)
        split_pieces.append(
            holding_tensor(
                lax.slice_in_dim(input_tensor, 0, shift_amount, 1, dimension_number), -start_offset
            )
        )
        covered += shift_amount
        start_offset += 1
    return jnp.concatenate(split_pieces, dimension_number)


def preceding_panel(input_tensor, dimension_number, border_extent, holding_tensor):
    axis_length = input_tensor.shape[dimension_number]
    split_pieces = [input_tensor]
    covered = 0
    start_offset = 1
    while covered < border_extent:
        shift_amount = min(axis_length, border_extent - covered)
        split_pieces.insert(
            0,
            holding_tensor(
                lax.slice_in_dim(
                    input_tensor, axis_length - shift_amount, axis_length, 1, dimension_number
                ),
                start_offset,
            ),
        )
        covered += shift_amount
        start_offset += 1
    return jnp.concatenate(split_pieces, dimension_number)


def forward_level(volume):
    planes, number_of_lines, col_count = (volume.shape[0], volume.shape[2], volume.shape[3])
    lowband, highband = analyse(following_panel(volume, 0, lead_taps, z_shift), 0, planes)
    banded = merge_bands(lowband, highband)
    lowband, highband = analyse(following_panel(banded, 2, lead_taps, y_shift), 2, number_of_lines)
    banded = merge_bands(lowband, highband)
    lowband, highband = analyse(wrap_ahead(banded, 3, lead_taps), 3, col_count)
    return merge_bands(lowband, highband)


def synth_x(current):
    lowband, highband = split_bands(current)
    return synthesise(
        wrap_behind(lowband, 3, trail_taps),
        wrap_behind(highband, 3, trail_taps),
        3,
        current.shape[3],
    )


def synth_y(extended, number_of_lines):
    lowband, highband = split_bands(extended)
    return synthesise(lowband, highband, 2, number_of_lines)


def synth_z(extended, planes):
    lowband, highband = split_bands(extended)
    return synthesise(lowband, highband, 0, planes)


def inverse_level(coeffs):
    planes, number_of_lines = (coeffs.shape[0], coeffs.shape[2])
    current = synth_x(coeffs)
    current = synth_y(preceding_panel(current, 2, trail_taps, y_shift), number_of_lines)
    return synth_z(preceding_panel(current, 0, trail_taps, z_shift), planes)


def spread(details, approximation, limits):
    bounds = limits[None, :, None, None, None]
    widened = details[:, None]
    shrunk = widened - jnp.clip(widened, -bounds, bounds)
    complete = jnp.concatenate([approximation[:, :, None], shrunk], 2)
    return complete.reshape((complete.shape[0], complete.shape[1] * 8) + complete.shape[3:])


def body(noisy_cube, thresholds):
    planes, number_of_lines, col_count = noisy_cube.shape
    level_one = forward_level(noisy_cube[:, None])
    level_two = forward_level(level_one[:, :1])
    details_one = level_one[:, 1:]
    details_two = level_two[:, 1:]
    squares = thresholds * thresholds
    square_grid = squares[:, None, None, None, None]

    def weights(details):
        widened = details[None]
        return jnp.sum(square_grid / (square_grid + widened * widened), axis=(1, 2, 3, 4))

    zero_local = weights(details_one) + weights(details_two)
    zero_weight = lax.psum(zero_local, ("gz", "gy"))
    count_two = level_two.shape
    coarse_two = jnp.broadcast_to(
        level_two[:, :1], (count_two[0], thresholds.shape[0], count_two[2], count_two[3])
    )
    approximation = inverse_level(spread(details_two, coarse_two, thresholds))
    denoised = inverse_level(spread(details_one, approximation, thresholds))
    residual = lax.psum(
        jnp.sum((denoised - noisy_cube[:, None]) ** 2, axis=(0, 2, 3)), ("gz", "gy")
    )
    cell_count = planes * number_of_lines * col_count * lax.axis_size("gz") * lax.axis_size("gy")
    gcv_score = cell_count * residual / (zero_weight * zero_weight)
    return (denoised, gcv_score)


def solution(mesh):
    in_specs = (P(("cube", "gz"), "gy", None), P())
    out_specs = (P(("cube", "gz"), None, "gy", None), P("cube"))
    return jax.shard_map(body, mesh=mesh, in_specs=in_specs, out_specs=out_specs, check_vma=False)
```

profile of v0, /device:TPU:0, one launch (start us, length us, event | category | flops | bytes accessed | tf_op | source)
XLA Modules:
  0.0 137.7 jit_solution(2075834466004949712)
XLA Ops:
  0.6 6.1 %collective-permute-start = (f32[4,1,32,256]{3,2,0,1:T(8,128)}, f32[4,1,32,256]{3,2,0,1:T(8,128)S(1)}, u32[]{:S(2)}, u32[]{:S(2)}) collective-permute-start(f32[4,1,32,256]{3,2,0,1:T(8,128)} %bitcast.244), channel_id=1, source_target_pairs={{0,14},{2,0},{4,2},{6,4},{8,6},{10,8},{12,10},{14,12},{1,15},{3,1}... | collective-permute-start | bytes 393224 | tf_op jit(solution)/shard_map/ppermute | solution.py:23
  6.7 0.9 slice_bitcast_fusion.4
  7.6 0.4 collective-permute-start.1
  8.0 3.8 %collective-permute-done.1 = f32[2,1,32,256]{3,2,0,1:T(8,128)S(1)} collective-permute-done((f32[2,1,32,256]{3,2,0,1:T(8,128)S(1)}, f32[2,1,32,256]{3,2,0,1:T(8,128)S(1)}, u32[]{:S(2)}, u32[]{:S(2)}) %collective-permute-start.1) | collective-permute-done | bytes 65568 | tf_op jit(solution)/shard_map/ppermute | solution.py:23
  11.8 0.9 pad_maximum_fusion.5
  12.8 1.0 add_bitcast_fusion.11
  14.0 1.0 collective-permute-done.2
  15.8 2.3 %slice.438 = f32[2,4,16,128]{3,2,1,0:T(8,128)S(1)} slice(f32[2,4,16,256]{3,2,1,0:T(8,128)S(1)} %bitcast.249), slice={[0:2:1], [0:4:1], [0:16:1], [1:256:2]} | slice | bytes 131072 | tf_op jit(solution)/shard_map/slice | solution.py:30
  18.1 2.3 %slice.437 = f32[2,4,16,128]{3,2,1,0:T(8,128)S(1)} slice(f32[2,4,16,256]{3,2,1,0:T(8,128)S(1)} %bitcast.250), slice={[0:2:1], [0:4:1], [0:16:1], [0:255:2]} | slice | bytes 131072 | tf_op jit(solution)/shard_map/slice | solution.py:30
  20.5 2.3 %slice.445 = f32[2,4,16,128]{3,2,1,0:T(8,128)S(1)} slice(f32[2,4,16,262]{3,2,1,0:T(8,128)S(1)} %pad_maximum_fusion.9), slice={[0:2:1], [0:4:1], [0:16:1], [7:262:2]} | slice | bytes 131072 | tf_op jit(solution)/shard_map/slice | solution.py:30
  22.9 2.3 %slice.444 = f32[2,4,16,128]{3,2,1,0:T(8,128)S(1)} slice(f32[2,4,16,262]{3,2,1,0:T(8,128)S(1)} %pad_maximum_fusion.9), slice={[0:2:1], [0:4:1], [0:16:1], [6:261:2]} | slice | bytes 131072 | tf_op jit(solution)/shard_map/slice | solution.py:30
  25.2 2.3 %slice.443 = f32[2,4,16,128]{3,2,1,0:T(8,128)S(1)} slice(f32[2,4,16,262]{3,2,1,0:T(8,128)S(1)} %pad_maximum_fusion.9), slice={[0:2:1], [0:4:1], [0:16:1], [5:260:2]} | slice | bytes 131072 | tf_op jit(solution)/shard_map/slice | solution.py:30
  27.5 2.3 %slice.442 = f32[2,4,16,128]{3,2,1,0:T(8,128)S(1)} slice(f32[2,4,16,262]{3,2,1,0:T(8,128)S(1)} %pad_maximum_fusion.9), slice={[0:2:1], [0:4:1], [0:16:1], [4:259:2]} | slice | bytes 131072 | tf_op jit(solution)/shard_map/slice | solution.py:30
  29.9 2.3 %slice.441 = f32[2,4,16,128]{3,2,1,0:T(8,128)S(1)} slice(f32[2,4,16,262]{3,2,1,0:T(8,128)S(1)} %pad_maximum_fusion.9), slice={[0:2:1], [0:4:1], [0:16:1], [3:258:2]} | slice | bytes 131072 | tf_op jit(solution)/shard_map/slice | solution.py:30
  32.2 2.3 %slice.440 = f32[2,4,16,128]{3,2,1,0:T(8,128)S(1)} slice(f32[2,4,16,262]{3,2,1,0:T(8,128)S(1)} %pad_maximum_fusion.9), slice={[0:2:1], [0:4:1], [0:16:1], [2:257:2]} | slice | bytes 131072 | tf_op jit(solution)/shard_map/slice | solution.py:30
  34.7 0.9 collective-permute-start.5
  35.7 2.7 %collective-permute-start.4 = (f32[2,1,16,128]{3,2,1,0:T(8,128)S(1)}, f32[2,1,16,128]{3,2,1,0:T(8,128)S(1)}, u32[]{:S(2)}, u32[]{:S(2)}) collective-permute-start(f32[2,1,16,128]{3,2,1,0:T(8,128)S(1)} %slice.541), channel_id=1, source_target_pairs={{0,12},{2,14},{4,0},{6,2},{8,4},{10,6},{12,8},{14,10},{1,13},{3,15... | collective-permute-start | bytes 49160 | tf_op jit(solution)/shard_map/ppermute | solution.py:23
  38.6 0.8 collective-permute-done.5
  39.4 1.3 collective-permute-done.4
  40.7 1.3 collective-permute-done.3
  42.2 1.1 collective-permute-done.6
  44.2 0.3 slice.472
  44.5 0.3 slice.471
  44.9 0.3 slice.470
  45.2 0.3 slice.469
  45.5 0.3 slice.468
  45.9 0.3 slice.467
  46.6 0.4 add_bitcast_fusion.5
  47.6 0.6 copy.325
  48.5 0.5 collective-permute-done.7
  49.2 3.8 %collective-permute-start.10 = (f32[1,8,16,128]{3,1,2,0:T(8,128)S(1)}, f32[1,8,16,128]{3,1,2,0:T(8,128)S(1)}, u32[]{:S(2)}, u32[]{:S(2)}) collective-permute-start(f32[1,8,16,128]{3,1,2,0:T(8,128)S(1)} %bitcast.270), channel_id=1, source_target_pairs={{0,6},{2,8},{4,10},{6,12},{8,14},{10,0},{12,2},{14,4},{1,7},{3,9},... | collective-permute-start | bytes 196616 | tf_op jit(solution)/shard_map/ppermute | solution.py:23
  53.2 0.9 collective-permute-start.8
  54.1 2.6 %collective-permute-done.10 = f32[1,8,16,128]{3,1,2,0:T(8,128)S(1)} collective-permute-done((f32[1,8,16,128]{3,1,2,0:T(8,128)S(1)}, f32[1,8,16,128]{3,1,2,0:T(8,128)S(1)}, u32[]{:S(2)}, u32[]{:S(2)}) %collective-permute-start.10) | collective-permute-done | bytes 65568 | tf_op jit(solution)/shard_map/ppermute | solution.py:23
  56.8 2.5 %collective-permute-done.9 = f32[1,8,16,128]{3,1,2,0:T(8,128)S(1)} collective-permute-done((f32[1,8,16,128]{3,1,2,0:T(8,128)S(1)}, f32[1,8,16,128]{3,1,2,0:T(8,128)S(1)}, u32[]{:S(2)}, u32[]{:S(2)}) %collective-permute-start.9) | collective-permute-done | bytes 65568 | tf_op jit(solution)/shard_map/ppermute | solution.py:23
  59.3 1.1 collective-permute-done.8
  60.9 1.3 add_bitcast_fusion.3
  62.3 4.3 %copy.350 = f32[2,16,16,128,2]{2,1,4,3,0:T(8,128)} copy(f32[2,16,16,128,2]{3,2,1,0,4:T(8,128)S(1)} %pad_maximum_fusion.2) | data formatting | bytes 1048576 | tf_op jit(solution)/shard_map/stack | solution.py:56
  66.6 5.4 %slice.596 = f32[2,16,3,256]{2,1,3,0:T(8,128)} slice(f32[2,16,16,256]{2,1,3,0:T(8,128)} %bitcast.235), slice={[0:2], [0:16], [13:16], [0:256]} | slice | bytes 196608 | tf_op jit(solution)/shard_map/slice | solution.py:127
  72.0 3.5 %copy.351 = f32[2,16,3,256]{3,1,2,0:T(8,128)S(1)} copy(f32[2,16,3,256]{2,1,3,0:T(8,128)} %slice.596) | data formatting | bytes 196608 | tf_op jit(solution)/shard_map/slice | solution.py:127
  75.6 4.3 %copy.353 = f32[2,16,16,128,2]{2,4,3,1,0:T(2,128)} copy(f32[2,16,16,128,2]{3,2,1,0,4:T(8,128)S(1)} %pad_maximum_fusion.2) | data formatting | bytes 1048576 | tf_op jit(solution)/shard_map/stack | solution.py:56
  79.9 2.8 %copy.355 = f32[2,8,2,16,256]{4,3,1,0,2:T(8,128)S(1)} copy(f32[2,8,2,16,256]{3,4,2,1,0:T(8,128)} %bitcast.234) | data formatting | bytes 1048576 | tf_op jit(solution)/shard_map/concatenate | solution.py:135
  82.9 0.4 add_bitcast_fusion.1
  84.4 0.4 copy.356
  84.8 9.8 %collective-permute-done.13 = f32[1,8,32,256]{3,1,2,0:T(8,128)S(1)} collective-permute-done((f32[1,8,32,256]{3,1,2,0:T(8,128)S(1)}, f32[1,8,32,256]{3,1,2,0:T(8,128)S(1)}, u32[]{:S(2)}, u32[]{:S(2)}) %collective-permute-start.13) | collective-permute-done | bytes 262176 | tf_op jit(solution)/shard_map/ppermute | solution.py:23
  94.8 6.4 %collective-permute-done.12 = f32[2,8,32,256]{3,1,2,0:T(8,128)S(1)} collective-permute-done((f32[2,8,32,256]{3,1,2,0:T(8,128)S(1)}, f32[2,8,32,256]{3,1,2,0:T(8,128)S(1)}, u32[]{:S(2)}, u32[]{:S(2)}) %collective-permute-start.12) | collective-permute-done | bytes 524320 | tf_op jit(solution)/shard_map/ppermute | solution.py:23
  102.4 0.8 copy.380
  103.3 33.9 %all-reduce = (f32[4]{0:T(128)S(1)}, f32[4]{0:T(128)S(1)}) all-reduce(f32[4]{0:T(128)S(1)} %add.977, f32[4]{0:T(128)S(1)} %get-tuple-element.12), channel_id=1, replica_groups=mesh['cube'=2,'gz'=8,'gy'=2] {'gz','gy'}, use_global_device_ids=true, to_apply=%region_4.5 | all-reduce | flops 8 | bytes 64 | tf_op jit(solution)/shard_map/psum | solution.py:197
  137.2 0.5 multiply_divide_fusion
  (104 shorter events, 7.0 us)
Async XLA Ops:
  0.6 41.6 %copy-start.1 = (f32[4]{0:T(128)S(1)}, f32[4]{0:T(128)}, u32[]{:S(2)}) copy-start(f32[4]{0:T(128)} %param.3) | copy-start | bytes 52
  0.6 11.2 %collective-permute-start = (f32[4,1,32,256]{3,2,0,1:T(8,128)}, f32[4,1,32,256]{3,2,0,1:T(8,128)S(1)}, u32[]{:S(2)}, u32[]{:S(2)}) collective-permute-start(f32[4,1,32,256]{3,2,0,1:T(8,128)} %bitcast.244), channel_id=1, source_target_pairs={{0,14},{2,0},{4,2},{6,4},{8,6},{10,8},{12,10},{14,12},{1,15},{3,1}... | collective-permute-start | bytes 393224 | tf_op jit(solution)/shard_map/ppermute | solution.py:23
  7.6 4.3 %collective-permute-start.1 = (f32[2,1,32,256]{3,2,0,1:T(8,128)S(1)}, f32[2,1,32,256]{3,2,0,1:T(8,128)S(1)}, u32[]{:S(2)}, u32[]{:S(2)}) collective-permute-start(f32[2,1,32,256]{3,2,0,1:T(8,128)S(1)} %slice_bitcast_fusion.4), channel_id=1, source_target_pairs={{0,12},{2,14},{4,0},{6,2},{8,4},{10,6},{12,8},{14,10},{1,13},{3,15... | collective-permute-start | bytes 196616 | tf_op jit(solution)/shard_map/ppermute | solution.py:23
  13.8 1.3 collective-permute-start.2
  34.7 4.7 %collective-permute-start.5 = (f32[2,1,16,128]{3,2,1,0:T(8,128)S(1)}, f32[2,1,16,128]{3,2,1,0:T(8,128)S(1)}, u32[]{:S(2)}, u32[]{:S(2)}) collective-permute-start(f32[2,1,16,128]{3,2,1,0:T(8,128)S(1)} %slice.541), channel_id=1, source_target_pairs={{0,10},{2,12},{4,14},{6,0},{8,2},{10,4},{12,6},{14,8},{1,11},{3,13... | collective-permute-start | bytes 49160 | tf_op jit(solution)/shard_map/ppermute | solution.py:23
  35.7 5.1 %collective-permute-start.4 = (f32[2,1,16,128]{3,2,1,0:T(8,128)S(1)}, f32[2,1,16,128]{3,2,1,0:T(8,128)S(1)}, u32[]{:S(2)}, u32[]{:S(2)}) collective-permute-start(f32[2,1,16,128]{3,2,1,0:T(8,128)S(1)} %slice.541), channel_id=1, source_target_pairs={{0,12},{2,14},{4,0},{6,2},{8,4},{10,6},{12,8},{14,10},{1,13},{3,15... | collective-permute-start | bytes 49160 | tf_op jit(solution)/shard_map/ppermute | solution.py:23
  38.3 3.7 %collective-permute-start.3 = (f32[2,1,16,128]{3,2,1,0:T(8,128)S(1)}, f32[2,1,16,128]{3,2,1,0:T(8,128)S(1)}, u32[]{:S(2)}, u32[]{:S(2)}) collective-permute-start(f32[2,1,16,128]{3,2,1,0:T(8,128)S(1)} %slice.541), channel_id=1, source_target_pairs={{0,14},{2,0},{4,2},{6,4},{8,6},{10,8},{12,10},{14,12},{1,15},{3,1}... | collective-permute-start | bytes 49160 | tf_op jit(solution)/shard_map/ppermute | solution.py:23
  42.1 1.2 collective-permute-start.6
  47.4 1.6 %collective-permute-start.7 = (f32[1,16,3,128]{1,2,3,0:T(4,128)S(1)}, f32[1,16,3,128]{1,2,3,0:T(4,128)S(1)}, u32[]{:S(2)}, u32[]{:S(2)}) collective-permute-start(f32[1,16,3,128]{1,2,3,0:T(4,128)S(1)} %slice.564), channel_id=1, source_target_pairs={{0,1},{1,0},{2,3},{3,2},{4,5},{5,4},{6,7},{7,6},{8,9},{9,8},{10,11... | collective-permute-start | bytes 73736 | tf_op jit(solution)/shard_map/ppermute | solution.py:23
  49.2 7.5 %collective-permute-start.10 = (f32[1,8,16,128]{3,1,2,0:T(8,128)S(1)}, f32[1,8,16,128]{3,1,2,0:T(8,128)S(1)}, u32[]{:S(2)}, u32[]{:S(2)}) collective-permute-start(f32[1,8,16,128]{3,1,2,0:T(8,128)S(1)} %bitcast.270), channel_id=1, source_target_pairs={{0,6},{2,8},{4,10},{6,12},{8,14},{10,0},{12,2},{14,4},{1,7},{3,9},... | collective-permute-start | bytes 196616 | tf_op jit(solution)/shard_map/ppermute | solution.py:23
  53.2 6.1 %collective-permute-start.9 = (f32[1,8,16,128]{3,1,2,0:T(8,128)S(1)}, f32[1,8,16,128]{3,1,2,0:T(8,128)S(1)}, u32[]{:S(2)}, u32[]{:S(2)}) collective-permute-start(f32[1,8,16,128]{3,1,2,0:T(8,128)S(1)} %bitcast.271), channel_id=1, source_target_pairs={{0,4},{2,6},{4,8},{6,10},{8,12},{10,14},{12,0},{14,2},{1,5},{3,7},... | collective-permute-start | bytes 196616 | tf_op jit(solution)/shard_map/ppermute | solution.py:23
  53.2 7.2 %collective-permute-start.8 = (f32[1,8,16,128]{3,1,2,0:T(8,128)S(1)}, f32[1,8,16,128]{3,1,2,0:T(8,128)S(1)}, u32[]{:S(2)}, u32[]{:S(2)}) collective-permute-start(f32[1,8,16,128]{3,1,2,0:T(8,128)S(1)} %bitcast.272), channel_id=1, source_target_pairs={{0,2},{2,4},{4,6},{6,8},{8,10},{10,12},{12,14},{14,0},{1,3},{3,5},... | collective-permute-start | bytes 196616 | tf_op jit(solution)/shard_map/ppermute | solution.py:23
  75.5 7.2 %collective-permute-start.11 = (f32[2,16,3,256]{3,1,2,0:T(8,128)S(1)}, f32[2,16,3,256]{3,1,2,0:T(8,128)S(1)}, u32[]{:S(2)}, u32[]{:S(2)}) collective-permute-start(f32[2,16,3,256]{3,1,2,0:T(8,128)S(1)} %copy.351), channel_id=1, source_target_pairs={{0,1},{1,0},{2,3},{3,2},{4,5},{5,4},{6,7},{7,6},{8,9},{9,8},{10,11... | collective-permute-start | bytes 294920 | tf_op jit(solution)/shard_map/ppermute | solution.py:23
  83.6 17.5 %collective-permute-start.12 = (f32[2,8,32,256]{3,1,2,0:T(8,128)S(1)}, f32[2,8,32,256]{3,1,2,0:T(8,128)S(1)}, u32[]{:S(2)}, u32[]{:S(2)}) collective-permute-start(f32[2,8,32,256]{3,1,2,0:T(8,128)S(1)} %bitcast.258), channel_id=1, source_target_pairs={{0,2},{2,4},{4,6},{6,8},{8,10},{10,12},{12,14},{14,0},{1,3},{3,5},... | collective-permute-start | bytes 1572872 | tf_op jit(solution)/shard_map/ppermute | solution.py:23
  84.1 10.5 %collective-permute-start.13 = (f32[1,8,32,256]{3,1,2,0:T(8,128)S(1)}, f32[1,8,32,256]{3,1,2,0:T(8,128)S(1)}, u32[]{:S(2)}, u32[]{:S(2)}) collective-permute-start(f32[1,8,32,256]{3,1,2,0:T(8,128)S(1)} %bitcast.269), channel_id=1, source_target_pairs={{0,4},{2,6},{4,8},{6,10},{8,12},{10,14},{12,0},{14,2},{1,5},{3,7},... | collective-permute-start | bytes 786440 | tf_op jit(solution)/shard_map/ppermute | solution.py:23
  101.3 0.9 copy-start
where the time goes:
time: 138 us
  local copies, waits for them, and re-layouts  48 us (35%)
  blocking collectives  33.9 us (25%)
  waiting for transfers between devices  32.3 us (23%)
  starting transfers between devices  15.7 us (11%)
  other arithmetic  6.35 us (5%)
  between operations  1.4 us (1%)
    psum x1, blocking collectives, body(): zero_weight = lax.psum(zero_local, ('gz', 'gy'))  33.9 us
    ppermute x14, waiting for transfers between devices, passed_along(): lax.ppermute(array, axis, [(i, (i + by) % devices) for i in range(devices)])  32.3 us
    slice x32, local copies, waits for them, and re-layouts, analyse(): lax.slice_in_dim(extended, tap_index, tap_index + axis_length - 1, 2, dim...  22.2 us
    ppermute x14, starting transfers between devices, passed_along(): lax.ppermute(array, axis, [(i, (i + by) % devices) for i in range(devices)])  15.7 us
    another operation x8, local copies, waits for them, and re-layouts, synthesise(): paired = jnp.stack([even_part, odd_part], dimension_number + 1)  11.1 us
    slice x4, local copies, waits for them, and re-layouts, preceding_panel(): lax.slice_in_dim(input_tensor, axis_length - shift_amount, axis_length, 1...  9.12 us
    concatenate x5, local copies, waits for them, and re-layouts, preceding_panel(): return jnp.concatenate(split_pieces, dimension_number)  3.26 us
  transfers between devices with their start and end apart: 14, of which 12 were waited for; matrix products, arithmetic and copies ran while one was open for 8% of the time, Pallas kernels for 0%

commit v1 on v0

--- a/solution.py
+++ b/solution.py
@@ -194,7 +194,7 @@
         return jnp.sum(square_grid / (square_grid + widened * widened), axis=(1, 2, 3, 4))
 
     zero_local = weights(details_one) + weights(details_two)
-    zero_weight = lax.psum(zero_local, ("gz", "gy"))
+    zero_weight = lax.psum(lax.psum(zero_local, "gy"), "gz")
     count_two = level_two.shape
     coarse_two = jnp.broadcast_to(
         level_two[:, :1], (count_two[0], thresholds.shape[0], count_two[2], count_two[3])

time: 138 us -> 149 us (1.080)
  blocking collectives: 33.9 us -> 60.8 us
  waiting for transfers between devices: 32.3 us -> 16.1 us
    psum x1 -> x3, blocking collectives: 33.9 us -> 60.8 us  [the longest x2 31.3 us: body(): zero_weight = lax.psum(lax.psum(zero_local, 'gy'), 'gz')]
    ppermute x14, waiting for transfers between devices: 32.3 us -> 16.1 us  [passed_along(): lax.ppermute(array, axis, [(i, (i + by) % devices) for i in range(devices)])]
  transfers between devices with their start and end apart: 14 -> 14, of which waited for: 12 -> 10; matrix products, arithmetic and copies ran while one was open for 8% -> 7% of each run, Pallas kernels for 0% -> 0%
where the time goes in v1:
time: 149 us; the launch traced here: 148 us
  blocking collectives  60.8 us (41%)
  local copies, waits for them, and re-layouts  48 us (32%)
  waiting for transfers between devices  16.1 us (11%)
  starting transfers between devices  15.7 us (11%)
  other arithmetic  6.34 us (4%)
    psum x2, blocking collectives, body(): zero_weight = lax.psum(lax.psum(zero_local, 'gy'), 'gz')  31.3 us
    psum x1, blocking collectives, body(): lax.psum(jnp.sum((denoised - noisy_cube[:, None]) ** 2, axis=(0, 2, 3)),...  29.5 us
    slice x32, local copies, waits for them, and re-layouts, analyse(): lax.slice_in_dim(extended, tap_index, tap_index + axis_length - 1, 2, dim...  22.2 us
    ppermute x14, waiting for transfers between devices, passed_along(): lax.ppermute(array, axis, [(i, (i + by) % devices) for i in range(devices)])  16.1 us
    ppermute x14, starting transfers between devices, passed_along(): lax.ppermute(array, axis, [(i, (i + by) % devices) for i in range(devices)])  15.7 us
    another operation x8, local copies, waits for them, and re-layouts, synthesise(): paired = jnp.stack([even_part, odd_part], dimension_number + 1)  11.1 us
    slice x4, local copies, waits for them, and re-layouts, preceding_panel(): lax.slice_in_dim(input_tensor, axis_length - shift_amount, axis_length, 1...  9.08 us
    concatenate x5, local copies, waits for them, and re-layouts, preceding_panel(): return jnp.concatenate(split_pieces, dimension_number)  3.26 us
  transfers between devices with their start and end apart: 14, of which 10 were waited for; matrix products, arithmetic and copies ran while one was open for 7% of the time, Pallas kernels for 0%

profile of v1, /device:TPU:0, one launch (start us, length us, event | category | flops | bytes accessed | tf_op | source)
XLA Modules:
  0.0 148.3 jit_solution(10336815150046521559)
XLA Ops:
  0.6 6.1 %collective-permute-start = (f32[4,1,32,256]{3,2,0,1:T(8,128)}, f32[4,1,32,256]{3,2,0,1:T(8,128)S(1)}, u32[]{:S(2)}, u32[]{:S(2)}) collective-permute-start(f32[4,1,32,256]{3,2,0,1:T(8,128)} %bitcast.244), channel_id=1, source_target_pairs={{0,14},{2,0},{4,2},{6,4},{8,6},{10,8},{12,10},{14,12},{1,15},{3,1}... | collective-permute-start | bytes 393224 | tf_op jit(solution)/shard_map/ppermute | solution.py:23
  6.7 0.9 slice_bitcast_fusion.4
  7.6 0.4 collective-permute-start.1
  8.0 3.8 %collective-permute-done.1 = f32[2,1,32,256]{3,2,0,1:T(8,128)S(1)} collective-permute-done((f32[2,1,32,256]{3,2,0,1:T(8,128)S(1)}, f32[2,1,32,256]{3,2,0,1:T(8,128)S(1)}, u32[]{:S(2)}, u32[]{:S(2)}) %collective-permute-start.1) | collective-permute-done | bytes 65568 | tf_op jit(solution)/shard_map/ppermute | solution.py:23
  11.8 0.9 pad_maximum_fusion.5
  12.8 1.0 add_bitcast_fusion.11
  14.0 1.0 collective-permute-done.2
  15.8 2.3 %slice.438 = f32[2,4,16,128]{3,2,1,0:T(8,128)S(1)} slice(f32[2,4,16,256]{3,2,1,0:T(8,128)S(1)} %bitcast.249), slice={[0:2:1], [0:4:1], [0:16:1], [1:256:2]} | slice | bytes 131072 | tf_op jit(solution)/shard_map/slice | solution.py:30
  18.1 2.3 %slice.437 = f32[2,4,16,128]{3,2,1,0:T(8,128)S(1)} slice(f32[2,4,16,256]{3,2,1,0:T(8,128)S(1)} %bitcast.250), slice={[0:2:1], [0:4:1], [0:16:1], [0:255:2]} | slice | bytes 131072 | tf_op jit(solution)/shard_map/slice | solution.py:30
  20.5 2.3 %slice.445 = f32[2,4,16,128]{3,2,1,0:T(8,128)S(1)} slice(f32[2,4,16,262]{3,2,1,0:T(8,128)S(1)} %pad_maximum_fusion.9), slice={[0:2:1], [0:4:1], [0:16:1], [7:262:2]} | slice | bytes 131072 | tf_op jit(solution)/shard_map/slice | solution.py:30
  22.9 2.3 %slice.444 = f32[2,4,16,128]{3,2,1,0:T(8,128)S(1)} slice(f32[2,4,16,262]{3,2,1,0:T(8,128)S(1)} %pad_maximum_fusion.9), slice={[0:2:1], [0:4:1], [0:16:1], [6:261:2]} | slice | bytes 131072 | tf_op jit(solution)/shard_map/slice | solution.py:30
  25.2 2.3 %slice.443 = f32[2,4,16,128]{3,2,1,0:T(8,128)S(1)} slice(f32[2,4,16,262]{3,2,1,0:T(8,128)S(1)} %pad_maximum_fusion.9), slice={[0:2:1], [0:4:1], [0:16:1], [5:260:2]} | slice | bytes 131072 | tf_op jit(solution)/shard_map/slice | solution.py:30
  27.5 2.3 %slice.442 = f32[2,4,16,128]{3,2,1,0:T(8,128)S(1)} slice(f32[2,4,16,262]{3,2,1,0:T(8,128)S(1)} %pad_maximum_fusion.9), slice={[0:2:1], [0:4:1], [0:16:1], [4:259:2]} | slice | bytes 131072 | tf_op jit(solution)/shard_map/slice | solution.py:30
  29.9 2.3 %slice.441 = f32[2,4,16,128]{3,2,1,0:T(8,128)S(1)} slice(f32[2,4,16,262]{3,2,1,0:T(8,128)S(1)} %pad_maximum_fusion.9), slice={[0:2:1], [0:4:1], [0:16:1], [3:258:2]} | slice | bytes 131072 | tf_op jit(solution)/shard_map/slice | solution.py:30
  32.2 2.3 %slice.440 = f32[2,4,16,128]{3,2,1,0:T(8,128)S(1)} slice(f32[2,4,16,262]{3,2,1,0:T(8,128)S(1)} %pad_maximum_fusion.9), slice={[0:2:1], [0:4:1], [0:16:1], [2:257:2]} | slice | bytes 131072 | tf_op jit(solution)/shard_map/slice | solution.py:30
  34.7 0.9 collective-permute-start.5
  35.7 2.7 %collective-permute-start.4 = (f32[2,1,16,128]{3,2,1,0:T(8,128)S(1)}, f32[2,1,16,128]{3,2,1,0:T(8,128)S(1)}, u32[]{:S(2)}, u32[]{:S(2)}) collective-permute-start(f32[2,1,16,128]{3,2,1,0:T(8,128)S(1)} %slice.541), channel_id=1, source_target_pairs={{0,12},{2,14},{4,0},{6,2},{8,4},{10,6},{12,8},{14,10},{1,13},{3,15... | collective-permute-start | bytes 49160 | tf_op jit(solution)/shard_map/ppermute | solution.py:23
  38.6 0.8 collective-permute-done.5
  39.4 1.3 collective-permute-done.4
  40.7 1.3 collective-permute-done.3
  42.2 1.1 collective-permute-done.6
  44.2 0.3 slice.472
  44.5 0.3 slice.471
  44.9 0.3 slice.470
  45.2 0.3 slice.469
  45.5 0.3 slice.468
  45.9 0.3 slice.467
  46.6 0.4 add_bitcast_fusion.5
  47.6 0.6 copy.325
  48.5 0.5 collective-permute-done.7
  49.2 3.8 %collective-permute-start.10 = (f32[1,8,16,128]{3,1,2,0:T(8,128)S(1)}, f32[1,8,16,128]{3,1,2,0:T(8,128)S(1)}, u32[]{:S(2)}, u32[]{:S(2)}) collective-permute-start(f32[1,8,16,128]{3,1,2,0:T(8,128)S(1)} %bitcast.270), channel_id=1, source_target_pairs={{0,6},{2,8},{4,10},{6,12},{8,14},{10,0},{12,2},{14,4},{1,7},{3,9},... | collective-permute-start | bytes 196616 | tf_op jit(solution)/shard_map/ppermute | solution.py:23
  53.2 0.9 collective-permute-start.8
  54.1 2.6 %collective-permute-done.10 = f32[1,8,16,128]{3,1,2,0:T(8,128)S(1)} collective-permute-done((f32[1,8,16,128]{3,1,2,0:T(8,128)S(1)}, f32[1,8,16,128]{3,1,2,0:T(8,128)S(1)}, u32[]{:S(2)}, u32[]{:S(2)}) %collective-permute-start.10) | collective-permute-done | bytes 65568 | tf_op jit(solution)/shard_map/ppermute | solution.py:23
  56.8 2.5 %collective-permute-done.9 = f32[1,8,16,128]{3,1,2,0:T(8,128)S(1)} collective-permute-done((f32[1,8,16,128]{3,1,2,0:T(8,128)S(1)}, f32[1,8,16,128]{3,1,2,0:T(8,128)S(1)}, u32[]{:S(2)}, u32[]{:S(2)}) %collective-permute-start.9) | collective-permute-done | bytes 65568 | tf_op jit(solution)/shard_map/ppermute | solution.py:23
  59.3 1.1 collective-permute-done.8
  60.9 1.3 add_bitcast_fusion.3
  62.3 4.4 %copy.350 = f32[2,16,16,128,2]{2,1,4,3,0:T(8,128)} copy(f32[2,16,16,128,2]{3,2,1,0,4:T(8,128)S(1)} %pad_maximum_fusion.2) | data formatting | bytes 1048576 | tf_op jit(solution)/shard_map/stack | solution.py:56
  66.6 5.3 %slice.596 = f32[2,16,3,256]{2,1,3,0:T(8,128)} slice(f32[2,16,16,256]{2,1,3,0:T(8,128)} %bitcast.235), slice={[0:2], [0:16], [13:16], [0:256]} | slice | bytes 196608 | tf_op jit(solution)/shard_map/slice | solution.py:127
  71.9 3.5 %copy.351 = f32[2,16,3,256]{3,1,2,0:T(8,128)S(1)} copy(f32[2,16,3,256]{2,1,3,0:T(8,128)} %slice.596) | data formatting | bytes 196608 | tf_op jit(solution)/shard_map/slice | solution.py:127
  75.6 4.3 %copy.353 = f32[2,16,16,128,2]{2,4,3,1,0:T(2,128)} copy(f32[2,16,16,128,2]{3,2,1,0,4:T(8,128)S(1)} %pad_maximum_fusion.2) | data formatting | bytes 1048576 | tf_op jit(solution)/shard_map/stack | solution.py:56
  79.9 2.8 %copy.355 = f32[2,8,2,16,256]{4,3,1,0,2:T(8,128)S(1)} copy(f32[2,8,2,16,256]{3,4,2,1,0:T(8,128)} %bitcast.234) | data formatting | bytes 1048576 | tf_op jit(solution)/shard_map/concatenate | solution.py:135
  82.9 0.4 add_bitcast_fusion.1
  84.4 2.6 %psum.22 = f32[4]{0:T(128)S(1)} all-reduce(f32[4]{0:T(128)S(1)} %add.979), channel_id=1, replica_groups=mesh['cube'=2,'gz'=8,'gy'=2] {'gy'}, use_global_device_ids=true, to_apply=%region_4.5 | all-reduce | flops 4 | bytes 32 | tf_op jit(solution)/shard_map/psum | solution.py:197
  87.0 28.7 %psum.23 = f32[4]{0:T(128)S(1)} all-reduce(f32[4]{0:T(128)S(1)} %psum.22), channel_id=1, replica_groups=mesh['cube'=2,'gz'=8,'gy'=2] {'gz'}, use_global_device_ids=true, to_apply=%region_5.6 | all-reduce | flops 4 | bytes 32 | tf_op jit(solution)/shard_map/psum | solution.py:197
  115.7 0.4 copy.356
  117.5 29.5 %psum.21 = f32[4]{0:T(128)S(1)} all-reduce(f32[4]{0:T(128)S(1)} %get-tuple-element.10), channel_id=1, replica_groups=mesh['cube'=2,'gz'=8,'gy'=2] {'gz','gy'}, use_global_device_ids=true, to_apply=%region_1.0 | all-reduce | flops 4 | bytes 32 | tf_op jit(solution)/shard_map/psum | solution.py:204
  147.0 0.8 copy.380
  147.8 0.5 multiply_divide_fusion
  (106 shorter events, 7.0 us)
Async XLA Ops:
  0.6 41.6 %copy-start.1 = (f32[4]{0:T(128)S(1)}, f32[4]{0:T(128)}, u32[]{:S(2)}) copy-start(f32[4]{0:T(128)} %param.3) | copy-start | bytes 52
  0.6 11.2 %collective-permute-start = (f32[4,1,32,256]{3,2,0,1:T(8,128)}, f32[4,1,32,256]{3,2,0,1:T(8,128)S(1)}, u32[]{:S(2)}, u32[]{:S(2)}) collective-permute-start(f32[4,1,32,256]{3,2,0,1:T(8,128)} %bitcast.244), channel_id=1, source_target_pairs={{0,14},{2,0},{4,2},{6,4},{8,6},{10,8},{12,10},{14,12},{1,15},{3,1}... | collective-permute-start | bytes 393224 | tf_op jit(solution)/shard_map/ppermute | solution.py:23
  7.6 4.3 %collective-permute-start.1 = (f32[2,1,32,256]{3,2,0,1:T(8,128)S(1)}, f32[2,1,32,256]{3,2,0,1:T(8,128)S(1)}, u32[]{:S(2)}, u32[]{:S(2)}) collective-permute-start(f32[2,1,32,256]{3,2,0,1:T(8,128)S(1)} %slice_bitcast_fusion.4), channel_id=1, source_target_pairs={{0,12},{2,14},{4,0},{6,2},{8,4},{10,6},{12,8},{14,10},{1,13},{3,15... | collective-permute-start | bytes 196616 | tf_op jit(solution)/shard_map/ppermute | solution.py:23
  13.8 1.3 collective-permute-start.2
  34.7 4.7 %collective-permute-start.5 = (f32[2,1,16,128]{3,2,1,0:T(8,128)S(1)}, f32[2,1,16,128]{3,2,1,0:T(8,128)S(1)}, u32[]{:S(2)}, u32[]{:S(2)}) collective-permute-start(f32[2,1,16,128]{3,2,1,0:T(8,128)S(1)} %slice.541), channel_id=1, source_target_pairs={{0,10},{2,12},{4,14},{6,0},{8,2},{10,4},{12,6},{14,8},{1,11},{3,13... | collective-permute-start | bytes 49160 | tf_op jit(solution)/shard_map/ppermute | solution.py:23
  35.7 5.1 %collective-permute-start.4 = (f32[2,1,16,128]{3,2,1,0:T(8,128)S(1)}, f32[2,1,16,128]{3,2,1,0:T(8,128)S(1)}, u32[]{:S(2)}, u32[]{:S(2)}) collective-permute-start(f32[2,1,16,128]{3,2,1,0:T(8,128)S(1)} %slice.541), channel_id=1, source_target_pairs={{0,12},{2,14},{4,0},{6,2},{8,4},{10,6},{12,8},{14,10},{1,13},{3,15... | collective-permute-start | bytes 49160 | tf_op jit(solution)/shard_map/ppermute | solution.py:23
  38.3 3.7 %collective-permute-start.3 = (f32[2,1,16,128]{3,2,1,0:T(8,128)S(1)}, f32[2,1,16,128]{3,2,1,0:T(8,128)S(1)}, u32[]{:S(2)}, u32[]{:S(2)}) collective-permute-start(f32[2,1,16,128]{3,2,1,0:T(8,128)S(1)} %slice.541), channel_id=1, source_target_pairs={{0,14},{2,0},{4,2},{6,4},{8,6},{10,8},{12,10},{14,12},{1,15},{3,1}... | collective-permute-start | bytes 49160 | tf_op jit(solution)/shard_map/ppermute | solution.py:23
  42.1 1.2 collective-permute-start.6
  47.4 1.6 %collective-permute-start.7 = (f32[1,16,3,128]{1,2,3,0:T(4,128)S(1)}, f32[1,16,3,128]{1,2,3,0:T(4,128)S(1)}, u32[]{:S(2)}, u32[]{:S(2)}) collective-permute-start(f32[1,16,3,128]{1,2,3,0:T(4,128)S(1)} %slice.564), channel_id=1, source_target_pairs={{0,1},{1,0},{2,3},{3,2},{4,5},{5,4},{6,7},{7,6},{8,9},{9,8},{10,11... | collective-permute-start | bytes 73736 | tf_op jit(solution)/shard_map/ppermute | solution.py:23
  49.2 7.5 %collective-permute-start.10 = (f32[1,8,16,128]{3,1,2,0:T(8,128)S(1)}, f32[1,8,16,128]{3,1,2,0:T(8,128)S(1)}, u32[]{:S(2)}, u32[]{:S(2)}) collective-permute-start(f32[1,8,16,128]{3,1,2,0:T(8,128)S(1)} %bitcast.270), channel_id=1, source_target_pairs={{0,6},{2,8},{4,10},{6,12},{8,14},{10,0},{12,2},{14,4},{1,7},{3,9},... | collective-permute-start | bytes 196616 | tf_op jit(solution)/shard_map/ppermute | solution.py:23
  53.2 6.1 %collective-permute-start.9 = (f32[1,8,16,128]{3,1,2,0:T(8,128)S(1)}, f32[1,8,16,128]{3,1,2,0:T(8,128)S(1)}, u32[]{:S(2)}, u32[]{:S(2)}) collective-permute-start(f32[1,8,16,128]{3,1,2,0:T(8,128)S(1)} %bitcast.271), channel_id=1, source_target_pairs={{0,4},{2,6},{4,8},{6,10},{8,12},{10,14},{12,0},{14,2},{1,5},{3,7},... | collective-permute-start | bytes 196616 | tf_op jit(solution)/shard_map/ppermute | solution.py:23
  53.2 7.2 %collective-permute-start.8 = (f32[1,8,16,128]{3,1,2,0:T(8,128)S(1)}, f32[1,8,16,128]{3,1,2,0:T(8,128)S(1)}, u32[]{:S(2)}, u32[]{:S(2)}) collective-permute-start(f32[1,8,16,128]{3,1,2,0:T(8,128)S(1)} %bitcast.272), channel_id=1, source_target_pairs={{0,2},{2,4},{4,6},{6,8},{8,10},{10,12},{12,14},{14,0},{1,3},{3,5},... | collective-permute-start | bytes 196616 | tf_op jit(solution)/shard_map/ppermute | solution.py:23
  75.5 7.2 %collective-permute-start.11 = (f32[2,16,3,256]{3,1,2,0:T(8,128)S(1)}, f32[2,16,3,256]{3,1,2,0:T(8,128)S(1)}, u32[]{:S(2)}, u32[]{:S(2)}) collective-permute-start(f32[2,16,3,256]{3,1,2,0:T(8,128)S(1)} %copy.351), channel_id=1, source_target_pairs={{0,1},{1,0},{2,3},{3,2},{4,5},{5,4},{6,7},{7,6},{8,9},{9,8},{10,11... | collective-permute-start | bytes 294920 | tf_op jit(solution)/shard_map/ppermute | solution.py:23
  83.6 32.6 %collective-permute-start.12 = (f32[2,8,32,256]{3,1,2,0:T(8,128)S(1)}, f32[2,8,32,256]{3,1,2,0:T(8,128)S(1)}, u32[]{:S(2)}, u32[]{:S(2)}) collective-permute-start(f32[2,8,32,256]{3,1,2,0:T(8,128)S(1)} %bitcast.258), channel_id=1, source_target_pairs={{0,2},{2,4},{4,6},{6,8},{8,10},{10,12},{12,14},{14,0},{1,3},{3,5},... | collective-permute-start | bytes 1572872 | tf_op jit(solution)/shard_map/ppermute | solution.py:23
  84.1 32.0 %collective-permute-start.13 = (f32[1,8,32,256]{3,1,2,0:T(8,128)S(1)}, f32[1,8,32,256]{3,1,2,0:T(8,128)S(1)}, u32[]{:S(2)}, u32[]{:S(2)}) collective-permute-start(f32[1,8,32,256]{3,1,2,0:T(8,128)S(1)} %bitcast.269), channel_id=1, source_target_pairs={{0,4},{2,6},{4,8},{6,10},{8,12},{10,14},{12,0},{14,2},{1,5},{3,7},... | collective-permute-start | bytes 786440 | tf_op jit(solution)/shard_map/ppermute | solution.py:23
  116.4 0.9 copy-start
